TPU v7x, 8 devices: a whole 2x2x1 slice. The times are simulated.
8 devices in a mesh: batch: 2 (over z, y), seq: 4 (over x, core).
Axes of the slice: x: 2, y: 2, z: 1, core: 2. Of those that a mesh axis runs over, the one named last changes fastest.
Arguments:
- hidden: bfloat16 [64, 4, 6144], P('batch'), parts along dimension 0
- cache_lens: int32 [64], P('batch'), parts along dimension 0
- c_kv: bfloat16 [64, 16384, 512], P('batch', 'seq'), parts along dimension 0
- k_r: bfloat16 [64, 16384, 64], P('batch', 'seq'), parts along dimension 0
- w_uq: bfloat16 [6144, 64, 128], P(None, 'seq')
- w_qr: bfloat16 [6144, 64, 64], P(None, 'seq')
- w_uk: bfloat16 [64, 128, 512], P('seq')
- w_uv: bfloat16 [64, 512, 128], P('seq')
- w_o: bfloat16 [64, 128, 6144], P('seq')
Outputs:
- output: bfloat16 [64, 4, 6144], P('batch'), parts along dimension 0
There are 2 independent parts. A program takes and returns all parts, laid end to end along the dimension named above; an argument that names none is the same for every part.
All inputs are finite; a program needn't handle non-finite values.
Results may differ from a plain program's by a relative error of at most 0.00663798.
Values are sent between devices in bfloat16 or wider.
A program may use at most 1 GiB of HBM per device.

v0:
```python
import jax
import jax.numpy as jnp
from jax import lax
from jax.sharding import PartitionSpec as P

MASK_FILL = -1e30


def solution(mesh):
    def local_step(hidden, cache_lens, c_kv, k_r, w_uq, w_qr, w_uk, w_uv, w_o):
        score_scale = (w_uq.shape[2] + w_qr.shape[2]) ** -0.5
        q_nope = jnp.einsum("cre,eil->cril", hidden, w_uq, preferred_element_type=jnp.float32).astype(jnp.bfloat16)
        q_rope = jnp.einsum("cre,eis->cris", hidden, w_qr, preferred_element_type=jnp.float32).astype(jnp.bfloat16)
        q_lat = jnp.einsum("bqhk,hkc->bqhc", q_nope, w_uk, preferred_element_type=jnp.float32).astype(jnp.bfloat16)
        lat_all = lax.all_gather(q_lat, "seq", axis=2, tiled=True)
        rope_all = lax.all_gather(q_rope, "seq", axis=2, tiled=True)
        local_len = c_kv.shape[1]
        positions = lax.axis_index("seq") * local_len + jnp.arange(local_len)
        limits = cache_lens[:, None] + jnp.arange(hidden.shape[1])[None, :]
        visible = positions[None, None, None, :] <= limits[:, :, None, None]
        scores = (jnp.einsum("bqhc,btc->bqht", lat_all, c_kv, preferred_element_type=jnp.float32)
                  + jnp.einsum("bqhr,btr->bqht", rope_all, k_r, preferred_element_type=jnp.float32)) * score_scale
        scores = jnp.where(visible, scores, MASK_FILL)
        local_max = jnp.max(scores, axis=-1)
        weights = jnp.exp(scores - local_max[..., None])
        local_sum = jnp.sum(weights, axis=-1)
        o_part = jnp.einsum("bqht,btc->bqhc", weights.astype(jnp.bfloat16), c_kv, preferred_element_type=jnp.float32)
        global_max = lax.pmax(local_max, "seq")
        rescale = jnp.exp(local_max - global_max)
        o_sum = lax.psum_scatter(o_part * rescale[..., None], "seq", scatter_dimension=2, tiled=True)
        l_sum = lax.psum_scatter(local_sum * rescale, "seq", scatter_dimension=2, tiled=True)
        o_lat = (o_sum / l_sum[..., None]).astype(jnp.bfloat16)
        o_val = jnp.einsum("bqhc,hcv->bqhv", o_lat, w_uv, preferred_element_type=jnp.float32).astype(jnp.bfloat16)
        y_part = jnp.einsum("criw,iwe->cre", o_val, w_o, preferred_element_type=jnp.float32)
        y_sum = lax.psum(y_part, "seq")
        return (hidden.astype(jnp.float32) + y_sum).astype(jnp.bfloat16)

    specs_in = (P("batch", None, None), P("batch"), P("batch", "seq", None), P("batch", "seq", None),
                P(None, "seq", None), P(None, "seq", None), P("seq", None, None), P("seq", None, None),
                P("seq", None, None))
    return jax.shard_map(local_step, mesh=mesh, in_specs=specs_in, out_specs=P("batch", None, None), check_vma=False)
```

profile of v0, /device:TPU:0, one launch (start us, length us, event | category | flops | bytes accessed | tf_op | source)
XLA Modules:
  0.0 614.9 jit_solution(1418752118857808798)
XLA Ops:
  6.5 0.0 copy-start
  6.5 0.0 all-gather.5.cloned.1.call-start
  6.5 10.7 %fusion.43 = bf16[32,4,16,64]{3,0,2,1:T(8,128)(2,1)} fusion(bf16[6144,16,64]{0,2,1:T(8,128)(2,1)} %param.14, bf16[32,4,6144,1]{2,1,0,3:T(4,128)(2,1)} %bitcast.67), kind=kOutput, calls=%fused_computation.33 | convolution fusion | flops 1610743808 | bytes 14417920 | tf_op jit(solution)/shard_map/cre,eis->cris/dot_general | solution.py:13
  17.3 0.0 all-gather.5.cloned.1.call-update
  17.3 0.0 copy-start.2
  17.3 0.0 all-gather.3.cloned.1.call-start
  17.4 14.2 %fusion.48 = bf16[32,4,16,128]{3,0,2,1:T(8,128)(2,1)S(1)} fusion(bf16[6144,16,128]{2,1,0:T(8,128)(2,1)} %param.13, bf16[32,4,6144,1]{2,1,0,3:T(4,128)(2,1)} %bitcast.68), kind=kOutput, calls=%fused_computation.34 | convolution fusion | flops 3221487616 | bytes 27262976 | tf_op jit(solution)/shard_map/cre,eil->cril/dot_general | solution.py:12
  31.6 0.0 copy-done
  31.6 2.0 convert_bitcast_fusion
  33.6 0.0 all-gather.3.cloned.1.call-update
  33.6 0.2 reduce-scatter.2.cloned.1.call-start
  33.8 0.0 copy-done.2
  33.8 0.1 iota_add_fusion
  33.9 0.6 broadcast_compare_fusion
  34.6 5.2 all-gather.5.cloned.1.call-done
  39.8 51.4 %fusion.15 = f32[32,4,64,4096]{3,2,1,0:T(8,128)} fusion(bf16[32,4096,64]{1,2,0:T(8,128)(2,1)} %param.12, bf16[32,4,64,64]{3,0,2,1:T(8,128)(2,1)} %all-gather.5.cloned.1.call-done), kind=kOutput, calls=%fused_computation.14 | convolution fusion | flops 4294967296 | bytes 152043520 | tf_op jit(solution)/shard_map/bqhr,btr->bqht/dot_general | solution.py:22
  91.2 5.9 all-gather.3.cloned.1.call-done
  97.1 164.5 %fusion.64 = (f32[32,4,64]{2,1,0:T(4,128)S(1)}, f32[32,4,64,4096]{3,2,1,0:T(8,128)}) fusion(f32[32,4,64,4096]{3,2,1,0:T(8,128)} %fusion.15, bf16[32,4096,512]{2,1,0:T(8,128)(2,1)} %param.11, bf16[32,4,64,512]{3,0,1,2:T(8,128)(2,1)} %all-gather.3.cloned.1.call-done, pred[32,4,4096]{2,1,0:T(4,128)(4,1)S(1)} %broadcast_compare_fusion), kind=kOutput, calls=%fused_computation.43 | convolution fusion | flops 34493947904 | bytes 411598848 | tf_op jit(solution)/shard_map/bqhc,btc->bqht/dot_general | solution.py:21
  261.6 10.9 %pmax.7 = f32[32,4,64]{2,1,0:T(4,128)S(1)} all-reduce(f32[32,4,64]{2,1,0:T(4,128)S(1)} %get-tuple-element.7), channel_id=1, replica_groups=mesh['batch'=2,'seq'=4] {'seq'}, use_global_device_ids=true, to_apply=%region_1.2 | all-reduce | flops 8192 | bytes 65536 | tf_op jit(solution)/shard_map/pmax | solution.py:28
  272.5 41.0 %fusion.4 = f32[32,4,64]{2,1,0:T(4,128)S(1)} fusion(f32[32,4,64,4096]{3,2,1,0:T(8,128)} %get-tuple-element.8, f32[32,4,64]{2,1,0:T(4,128)S(1)} %get-tuple-element.7), kind=kLoop, calls=%fused_computation.6 | loop fusion | flops 67100672 | bytes 134283264 | tf_op jit(solution)/shard_map/reduce_sum | solution.py:26
  313.5 87.1 %fusion.19 = f32[32,4,64,512]{3,2,1,0:T(8,128)} fusion(bf16[32,4096,512]{2,1,0:T(8,128)(2,1)} %param.11, f32[32,4,64,4096]{3,2,1,0:T(8,128)} %get-tuple-element.8, f32[32,4,64]{2,1,0:T(4,128)S(1)} %get-tuple-element.7, f32[32,4,64]{2,1,0:T(4,128)S(1)} %bitcast.73), kind=kOutput, calls=%fused_computation.18 | convolution fusion | flops 34431041536 | bytes 285278208 | tf_op jit(solution)/shard_map/bqht,btc->bqhc/dot_general | solution.py:27
  400.6 0.0 copy-start.3
  400.6 0.0 reduce-scatter.2.cloned.1.call-update
  400.6 0.0 all-reduce.3.cloned.1.call-start
  400.7 0.6 copy-done.3
  401.3 0.6 dynamic-slice
  402.5 0.1 copy.35
  402.6 11.5 %all-reduce = f32[32,4,64]{0,1,2:T(4,128)S(1)} all-reduce(f32[32,4,64]{0,1,2:T(4,128)S(1)} %copy.35), channel_id=3, replica_groups=mesh['batch'=2,'seq'=4] {'seq'}, use_global_device_ids=true, to_apply=%region_4.5.clone | all-reduce | flops 8192 | bytes 65536
  414.2 0.1 copy.36
  414.3 106.3 %reduce-scatter.2.cloned.1.call-done = f32[32,4,16,512]{3,2,1,0:T(8,128)} async-done(((f32[32,4,64,512]{3,2,1,0:T(8,128)}), f32[32,4,16,512]{3,2,1,0:T(8,128)}) %reduce-scatter.2.cloned.1.call-update) | async-done | bytes 4194320 | tf_op jit(solution)/shard_map/reduce_scatter | solution.py:30
  520.6 3.9 divide_convert_fusion
  524.4 0.0 copy-start.1
  524.4 15.4 %fusion.25 = f32[32,4,6144]{2,0,1:T(8,128)} fusion(bf16[16,128,6144]{2,1,0:T(8,128)(2,1)} %param.17, bf16[16,512,128]{2,1,0:T(8,128)(2,1)} %param.16, bf16[32,4,16,512]{3,2,1,0:T(8,128)(2,1)} %divide_convert_fusion), kind=kOutput, calls=%fused_computation.20 | convolution fusion | flops 3489923072 | bytes 32505856 | tf_op jit(solution)/shard_map/criw,iwe->cre/dot_general | solution.py:34
  539.8 0.0 all-reduce.3.cloned.1.call-update
  539.8 62.9 %all-reduce.3.cloned.1.call-done = f32[32,4,6144]{2,0,1:T(8,128)} async-done(((f32[32,4,6144]{2,0,1:T(8,128)}), f32[32,4,6144]{2,0,1:T(8,128)}) %all-reduce.3.cloned.1.call-update) | async-done | bytes 3145744 | tf_op jit(solution)/shard_map/psum | solution.py:35
  602.7 3.3 add_convert_fusion
  606.1 2.4 copy.38
  608.4 0.0 copy-done.1
  (3 shorter events, 0.0 us)
Async XLA Ops:
  6.5 25.0 %copy-start = (bf16[16,128,512]{2,1,0:T(8,128)(2,1)S(1)}, bf16[16,128,512]{2,1,0:T(8,128)(2,1)}, u32[]{:S(2)}) copy-start(bf16[16,128,512]{2,1,0:T(8,128)(2,1)} %param.15) | copy-start | bytes 6291460
  6.5 33.3 %all-gather.5.cloned.1.call-start = ((), (), s32[]{:S(2)}) async-start(), calls=%async_computation.2 | async-start | bytes 2621440 | tf_op jit(solution)/shard_map/all_gather | solution.py:16
  17.3 16.5 %copy-start.2 = (s32[32]{0:T(128)S(1)}, s32[32]{0:T(128)}, u32[]{:S(2)}) copy-start(s32[32]{0:T(128)} %param.10) | copy-start | bytes 388
  17.3 79.8 %all-gather.3.cloned.1.call-start = ((), (), s32[]{:S(2)}) async-start(), calls=%async_computation.1 | async-start | bytes 10485760 | tf_op jit(solution)/shard_map/all_gather | solution.py:15
  33.6 487.0 %reduce-scatter.2.cloned.1.call-start = ((), (), s32[]{:S(2)}) async-start(), calls=%async_computation.3 | async-start | bytes 20971520 | tf_op jit(solution)/shard_map/reduce_scatter | solution.py:30
  400.6 0.7 copy-start.3
  400.6 202.1 %all-reduce.3.cloned.1.call-start = ((), (), s32[]{:S(2)}) async-start(), calls=%async_computation.4 | async-start | bytes 6291456 | tf_op jit(solution)/shard_map/psum | solution.py:35
  524.4 84.0 %copy-start.1 = (bf16[16,128,512]{2,1,0:T(8,128)(2,1)S(1)}, bf16[16,128,512]{2,1,0:T(8,128)(2,1)}, u32[]{:S(2)}) copy-start(bf16[16,128,512]{2,1,0:T(8,128)(2,1)} %param.15) | copy-start | bytes 6291460
Sparse Core Ops, SparseCore 0:
  17.4 22.3 all-gather.4
  41.3 55.7 all-gather.2
  400.7 119.7 reduce-scatter.1
  540.0 62.7 all-reduce.2
where the time goes:
time: 615 us
  matrix products  345 us (56%)
  waiting for transfers between devices  180 us (29%)
  other arithmetic  48.9 us (8%)
  blocking collectives  22.4 us (4%)
  between operations  13.9 us (2%)
    dot_general x1, matrix products, local_step(): jnp.einsum('bqhc,btc->bqht', lat_all, c_kv, preferred_element_type=jnp.fl...  164 us
    reduce_scatter x1, waiting for transfers between devices, local_step(): lax.psum_scatter(o_part * rescale[..., None], 'seq', scatter_dimension=2,...  106 us
    dot_general x1, matrix products, local_step(): jnp.einsum('bqht,btc->bqhc', weights.astype(jnp.bfloat16), c_kv, preferre...  87.1 us
    psum x1, waiting for transfers between devices, local_step(): y_sum = lax.psum(y_part, 'seq')  62.9 us
    dot_general x1, matrix products, local_step(): jnp.einsum('bqhr,btr->bqht', rope_all, k_r, preferred_element_type=jnp.fl...  51.4 us
    reduce_sum x1, other arithmetic, local_step(): local_sum = jnp.sum(weights, axis=-1)  41 us
    dot_general x1, matrix products, local_step(): jnp.einsum('criw,iwe->cre', o_val, w_o, preferred_element_type=jnp.float32)  15.4 us
    dot_general x1, matrix products, local_step(): jnp.einsum('cre,eil->cril', hidden, w_uq, preferred_element_type=jnp.floa...  14.2 us
  transfers between devices with their start and end apart: 4, of which 4 were waited for; matrix products, arithmetic and copies ran while one was open for 11% of the time, Pallas kernels for 0%

commit v1 on v0

v1 whole, which is shorter than its diff:
```python
import functools
import math

import jax
import jax.numpy as jnp
from jax import lax
from jax.experimental import pallas as pl
from jax.experimental.pallas import tpu as pltpu
from jax.sharding import PartitionSpec as P

MASK_FILL = -1e30
MESH = pl.DeviceIdType.MESH
CHUNK = 1024


def _attend_kernel(rows, toks, seq_len, score_scale, lens_ref, q_hbm, kv_hbm, kr_hbm, o_ref,
                   qbuf, kvbuf, krbuf, oacc, ostat, pbuf, pstat, xsend, xstat, xrecv, xrstat, own,
                   q_local, q_cross, q_side, q_fwd, kv_sem, kr_sem, p_sem, ps_sem, x_sem, xs_sem):
    me = lax.axis_index("seq")
    side = me + 1 - 2 * lax.rem(me, 2)
    cross = lax.rem(me + 2, 4)
    diag = lax.rem(side + 2, 4)
    pairs = rows // 2
    lat = kvbuf.shape[2]
    rope = kr_hbm.shape[1]
    group = qbuf.shape[2]
    queries = 4 * group

    def to(dev):
        return {"seq": dev}

    def kv_copies(row, slot):
        return (pltpu.make_async_copy(kv_hbm.at[row], kvbuf.at[slot], kv_sem.at[slot]),
                pltpu.make_async_copy(kr_hbm.at[row], krbuf.at[slot, pl.ds(pl.multiple_of(slot * rope, rope), rope)], kr_sem.at[slot]))

    def local_q(k):
        return pltpu.make_async_copy(q_hbm.at[k], qbuf.at[k, 0], q_local.at[k])

    def cross_q(k):
        return pltpu.make_async_remote_copy(q_hbm.at[k], qbuf.at[k, 1], q_cross.at[0, k], q_cross.at[1, k],
                                            device_id=to(cross), device_id_type=MESH)

    def side_q(k):
        return pltpu.make_async_remote_copy(q_hbm.at[k], qbuf.at[k, 2], q_side.at[0, k], q_side.at[1, k],
                                            device_id=to(side), device_id_type=MESH)

    def fwd_q(k):
        return pltpu.make_async_remote_copy(qbuf.at[k, 1], qbuf.at[k, 3], q_fwd.at[0, k], q_fwd.at[1, k],
                                            device_id=to(side), device_id_type=MESH)

    def side_o(row):
        slot, land = lax.rem(row, 2), lax.rem(row, 4)
        return (pltpu.make_async_remote_copy(oacc.at[slot, pl.ds(2 * group, 2 * group)], pbuf.at[land], p_sem.at[0, slot], p_sem.at[1, land],
                                             device_id=to(side), device_id_type=MESH),
                pltpu.make_async_remote_copy(ostat.at[slot, :, pl.ds(2 * group, 2 * group)], pstat.at[land], ps_sem.at[0, slot], ps_sem.at[1, land],
                                             device_id=to(side), device_id_type=MESH))

    def cross_o(row):
        return (pltpu.make_async_remote_copy(xsend.at[row], xrecv.at[row], x_sem.at[0, row], x_sem.at[1, row],
                                             device_id=to(cross), device_id_type=MESH),
                pltpu.make_async_remote_copy(xstat.at[row], xrstat.at[row], xs_sem.at[0, row], xs_sem.at[1, row],
                                             device_id=to(cross), device_id_type=MESH))

    for copy in kv_copies(0, 0):
        copy.start()
    local_q(0).start()
    barrier = pltpu.get_barrier_semaphore()
    for dev in (side, cross, diag):
        pl.semaphore_signal(barrier, inc=1, device_id=to(dev), device_id_type=MESH)
    pl.semaphore_wait(barrier, 3)

    def launch(k, carry):
        cross_q(k).start()
        side_q(k).start()

        @pl.when(k > 0)
        def _():
            local_q(k).start()
        return carry
    lax.fori_loop(0, pairs, launch, 0)
    krbuf[0, rope:, :] = jnp.zeros((rope, krbuf.shape[2]), krbuf.dtype)
    krbuf[1, :rope, :] = jnp.zeros((rope, krbuf.shape[2]), krbuf.dtype)

    def forward(k):
        cross_q(k).wait_recv()
        fwd_q(k).start()

    forward(0)
    fold = score_scale * math.log2(math.e)
    tok_of = lax.rem(lax.broadcasted_iota(jnp.int32, (queries, 1), 0), toks)
    lane_of = lax.broadcasted_iota(jnp.int32, (queries, CHUNK), 1)

    def attend(row, slot):
        pair = row // 2
        q_lat = qbuf[pair, :, :, pl.ds(pl.multiple_of(slot * lat, lat), lat)].reshape(queries, lat)
        q_rot = qbuf[pair, :, :, 2 * lat:].reshape(queries, 2 * rope)
        limit = lens_ref[row] - me * seq_len + tok_of
        top = total = acc = None
        for j in range(seq_len // CHUNK):
            part = kvbuf[slot, j * CHUNK:(j + 1) * CHUNK, :]
            s = lax.dot_general(q_lat, part, (((1,), (1,)), ((), ())), preferred_element_type=jnp.float32)
            s = s + jnp.dot(q_rot, krbuf[slot, :, j * CHUNK:(j + 1) * CHUNK], preferred_element_type=jnp.float32)
            s = jnp.where(lane_of <= limit - j * CHUNK, s * fold, MASK_FILL)
            peak = jnp.max(s, axis=1, keepdims=True)
            new_top = peak if top is None else jnp.maximum(top, peak)
            p = jnp.exp2(s - new_top)
            psum = jnp.sum(p, axis=1, keepdims=True)
            o = jnp.dot(p.astype(jnp.bfloat16), part, preferred_element_type=jnp.float32)
            if top is None:
                total, acc = psum, o
            else:
                keep = jnp.exp2(top - new_top)
                total = total * keep + psum
                acc = acc * keep + o
            top = new_top
        oacc[slot] = acc
        ostat[slot, 0] = jnp.broadcast_to(top, (queries, 128))
        ostat[slot, 1] = jnp.broadcast_to(total, (queries, 128))

    def merge_side(row):
        slot, land = lax.rem(row, 2), lax.rem(row, 4)
        for copy in side_o(row):
            copy.wait()
        top_a, top_b = ostat[slot, 0, :2 * group], pstat[land, 0]
        new_top = jnp.maximum(top_a, top_b)
        keep_a, keep_b = jnp.exp2(top_a - new_top), jnp.exp2(top_b - new_top)
        total = ostat[slot, 1, :2 * group] * keep_a + pstat[land, 1] * keep_b
        for n in range(lat // 128):
            cols = slice(n * 128, (n + 1) * 128)
            merged = oacc[slot, :2 * group, cols] * keep_a + pbuf[land, :, cols] * keep_b
            own[row, :, cols] = merged[:group]
            xsend[row, :, cols] = merged[group:]
        lane = lax.broadcasted_iota(jnp.int32, (2 * group, 128), 1)
        packed = jnp.transpose(jnp.where(lane == 0, new_top, total))
        xstat[row] = packed[:8]
        for copy in cross_o(row):
            copy.start()

    def body(row, carry):
        slot = lax.rem(row, 2)
        pair = row // 2

        @pl.when(row + 1 < rows)
        def _():
            for copy in kv_copies(row + 1, 1 - slot):
                copy.start()

        @pl.when(slot == 0)
        def _():
            local_q(pair).wait()
            side_q(pair).wait_recv()
            fwd_q(pair).wait_recv()

        @pl.when((slot == 1) & (pair + 1 < pairs))
        def _():
            forward(pair + 1)

        for copy in kv_copies(row, slot):
            copy.wait()
        attend(row, slot)
        for copy in side_o(row):
            copy.start()

        @pl.when(row > 0)
        def _():
            merge_side(row - 1)
        return carry

    lax.fori_loop(0, rows, body, 0)
    merge_side(rows - 1)

    def finish(row, carry):
        for copy in cross_o(row):
            copy.wait_recv()
        pad = jnp.zeros((120, 128), jnp.float32)
        mine = jnp.transpose(jnp.concatenate([xstat[row], pad], axis=0))[:group]
        theirs = jnp.transpose(jnp.concatenate([xrstat[row], pad], axis=0))[group:]
        top_a, top_b = mine[:, 0:1], theirs[:, 0:1]
        new_top = jnp.maximum(top_a, top_b)
        keep_a, keep_b = jnp.exp2(top_a - new_top), jnp.exp2(top_b - new_top)
        total = mine[:, 1:2] * keep_a + theirs[:, 1:2] * keep_b
        o_ref[row] = ((own[row] * keep_a + xrecv[row] * keep_b) / total).astype(o_ref.dtype)
        return carry
    lax.fori_loop(0, rows, finish, 0)

    def drain_q(k, carry):
        cross_q(k).wait_send()
        side_q(k).wait_send()
        fwd_q(k).wait_send()
        return carry
    lax.fori_loop(0, pairs, drain_q, 0)

    def drain_o(row, carry):
        for copy in cross_o(row):
            copy.wait_send()
        return carry
    lax.fori_loop(0, rows, drain_o, 0)


def _attend(lens, q_pack, c_kv, k_rt, toks, score_scale):
    rows, seq_len, lat = c_kv.shape
    rope = k_rt.shape[1]
    pairs, group, width = q_pack.shape
    f32, bf16 = jnp.float32, jnp.bfloat16
    dma = pltpu.SemaphoreType.DMA
    return pl.pallas_call(
        functools.partial(_attend_kernel, rows, toks, seq_len, score_scale),
        out_shape=jax.ShapeDtypeStruct((rows, group, lat), bf16),
        in_specs=[pl.BlockSpec(memory_space=pltpu.SMEM)] + [pl.BlockSpec(memory_space=pl.ANY)] * 3,
        out_specs=pl.BlockSpec(memory_space=pltpu.VMEM),
        scratch_shapes=[
            pltpu.VMEM((pairs, 4, group, width), bf16),
            pltpu.VMEM((2, seq_len, lat), bf16),
            pltpu.VMEM((2, 2 * rope, seq_len), bf16),
            pltpu.VMEM((2, 4 * group, lat), f32),
            pltpu.VMEM((2, 2, 4 * group, 128), f32),
            pltpu.VMEM((4, 2 * group, lat), f32),
            pltpu.VMEM((4, 2, 2 * group, 128), f32),
            pltpu.VMEM((rows, group, lat), f32),
            pltpu.VMEM((rows, 8, 128), f32),
            pltpu.VMEM((rows, group, lat), f32),
            pltpu.VMEM((rows, 8, 128), f32),
            pltpu.VMEM((rows, group, lat), f32),
            dma((pairs,)), dma((2, pairs)), dma((2, pairs)), dma((2, pairs)),
            dma((2,)), dma((2,)), dma((2, 4)), dma((2, 4)), dma((2, rows)), dma((2, rows)),
        ],
        compiler_params=pltpu.CompilerParams(collective_id=0, has_side_effects=True, vmem_limit_bytes=60 * 1024 * 1024),
        name="attend",
    )(lens, q_pack, c_kv, k_rt)


def solution(mesh):
    def local_step(hidden, cache_lens, c_kv, k_r, w_uq, w_qr, w_uk, w_uv, w_o):
        rows, toks, _ = hidden.shape
        heads, nope, lat = w_uk.shape
        rope = w_qr.shape[2]
        score_scale = (nope + rope) ** -0.5
        q_nope = jnp.einsum("cre,eil->cril", hidden, w_uq, preferred_element_type=jnp.float32).astype(jnp.bfloat16)
        q_rope = jnp.einsum("cre,eis->cris", hidden, w_qr, preferred_element_type=jnp.float32).astype(jnp.bfloat16)
        q_lat = jnp.einsum("bqhk,hkc->bqhc", q_nope, w_uk, preferred_element_type=jnp.float32).astype(jnp.bfloat16)
        q_lat = q_lat.reshape(rows // 2, 2, toks, heads, lat).transpose(0, 3, 2, 1, 4).reshape(rows // 2, heads * toks, 2 * lat)
        q_rope = q_rope.reshape(rows // 2, 2, toks, heads, rope).transpose(0, 3, 2, 1, 4).reshape(rows // 2, heads * toks, 2 * rope)
        q_pack = jnp.concatenate([q_lat, q_rope], axis=-1)
        o_lat = _attend(cache_lens, q_pack, c_kv, jnp.swapaxes(k_r, 1, 2), toks, score_scale)
        o_lat = o_lat.reshape(rows, heads, toks, lat).transpose(0, 2, 1, 3)
        o_val = jnp.einsum("bqhc,hcv->bqhv", o_lat, w_uv, preferred_element_type=jnp.float32).astype(jnp.bfloat16)
        y_part = jnp.einsum("criw,iwe->cre", o_val, w_o, preferred_element_type=jnp.float32)
        y_sum = lax.psum(y_part, "seq")
        return (hidden.astype(jnp.float32) + y_sum).astype(jnp.bfloat16)

    specs_in = (P("batch", None, None), P("batch"), P("batch", "seq", None), P("batch", "seq", None),
                P(None, "seq", None), P(None, "seq", None), P("seq", None, None), P("seq", None, None),
                P("seq", None, None))
    return jax.shard_map(local_step, mesh=mesh, in_specs=specs_in, out_specs=P("batch", None, None), check_vma=False)
```

time: 615 us -> 295 us (0.48)
  matrix products: 345 us -> 41.8 us
  Pallas kernels: 0 us -> 155 us
  waiting for transfers between devices: 180 us -> 64.4 us
  other arithmetic: 48.9 us -> 5.16 us
  blocking collectives: 22.4 us -> 0 us
  local copies, waits for them, and re-layouts: 3.75 us -> 15 us
    dot_general x3 -> x0, matrix products: 303 us -> none  [the longest x1 164 us: local_step(): jnp.einsum('bqhc,btc->bqht', lat_all, c_kv, preferred_element_type=jnp.fl...]
    pallas_call x0 -> x1, Pallas kernels: none -> 155 us  [_attend(): pl.pallas_call(functools.partial(_attend_kernel, rows, toks, seq_len, sco...]
    reduce_scatter x1 -> x0, waiting for transfers between devices: 106 us -> none  [local_step(): lax.psum_scatter(o_part * rescale[..., None], 'seq', scatter_dimension=2,...]
    reduce_sum x1 -> x0, other arithmetic: 41 us -> none  [local_step(): local_sum = jnp.sum(weights, axis=-1)]
    reshape x0 -> x6, local copies, waits for them, and re-layouts: none -> 12.6 us  [the longest x3 9.33 us: local_step(): q_lat.reshape(rows // 2, 2, toks, heads, lat).transpose(0, 3, 2, 1, 4)]
    unnamed x1 -> x0, blocking collectives: 11.5 us -> none
    all_gather x2 -> x0, waiting for transfers between devices: 11.1 us -> none  [the longest x1 5.89 us: local_step(): lat_all = lax.all_gather(q_lat, 'seq', axis=2, tiled=True)]
    pmax x1 -> x0, blocking collectives: 10.9 us -> none  [local_step(): global_max = lax.pmax(local_max, 'seq')]
  transfers between devices with their start and end apart: 4 -> 1, of which waited for: 4 -> 1; matrix products, arithmetic and copies ran while one was open for 11% -> 0% of each run, Pallas kernels for 0% -> 0%
where the time goes in v1:
time: 295 us; the launch traced here: 294 us
  Pallas kernels  155 us (53%)
  waiting for transfers between devices  64.4 us (22%)
  matrix products  41.8 us (14%)
  local copies, waits for them, and re-layouts  15 us (5%)
  between operations  13.5 us (5%)
  other arithmetic  5.16 us (2%)
    pallas_call x1, Pallas kernels, _attend(): pl.pallas_call(functools.partial(_attend_kernel, rows, toks, seq_len, sco...  155 us
    psum x1, waiting for transfers between devices, local_step(): y_sum = lax.psum(y_part, 'seq')  64.4 us
    dot_general x1, matrix products, local_step(): jnp.einsum('cre,eil->cril', hidden, w_uq, preferred_element_type=jnp.floa...  17.7 us
    dot_general x1, matrix products, local_step(): jnp.einsum('criw,iwe->cre', o_val, w_o, preferred_element_type=jnp.float32)  13.2 us
    reshape x3, local copies, waits for them, and re-layouts, local_step(): q_lat.reshape(rows // 2, 2, toks, heads, lat).transpose(0, 3, 2, 1, 4)  9.33 us
    dot_general x1, matrix products, local_step(): jnp.einsum('cre,eis->cris', hidden, w_qr, preferred_element_type=jnp.floa...  8.96 us
  transfers between devices with their start and end apart: 1, of which 1 were waited for; matrix products, arithmetic and copies ran while one was open for 0% of the time, Pallas kernels for 0%

profile of v1, /device:TPU:0, one launch (start us, length us, event | category | flops | bytes accessed | tf_op | source)
XLA Modules:
  0.0 294.4 jit_solution(2217050450549465657)
XLA Ops:
  6.5 0.0 copy-start
  6.5 0.0 all-reduce.2.cloned.1.call-start
  6.5 0.0 copy-start.2
  6.5 17.7 %fusion.28 = bf16[32,4,16,128]{3,0,1,2:T(8,128)(2,1)S(1)} fusion(bf16[6144,16,128,1]{2,1,0,3:T(8,128)(2,1)} %bitcast.59, bf16[32,4,6144,1]{2,1,0,3:T(4,128)(2,1)} %bitcast.56), kind=kOutput, calls=%fused_computation.20 | convolution fusion | flops 3221487616 | bytes 27262976 | tf_op jit(solution)/shard_map/cre,eil->cril/dot_general | solution.py:238
  24.2 0.0 copy-done.2
  24.3 9.0 %fusion.23 = bf16[32,4,16,64]{3,0,2,1:T(8,128)(2,1)S(1)} fusion(bf16[6144,16,64]{0,2,1:T(8,128)(2,1)} %param.14, bf16[32,4,6144,1]{2,1,0,3:T(4,128)(2,1)S(1)} %bitcast.57), kind=kOutput, calls=%fused_computation.19 | convolution fusion | flops 1610743808 | bytes 14417920 | tf_op jit(solution)/shard_map/cre,eis->cris/dot_general | solution.py:239
  33.2 0.5 copy.47
  33.7 0.2 reshape.18
  34.0 0.0 copy-done
  34.0 2.0 convert_bitcast_fusion
  36.0 2.7 reshape.15
  38.7 3.4 %copy.46 = bf16[16,2,4,16,512]{4,1,2,3,0:T(2,128)(2,1)} copy(bf16[16,2,4,16,512]{4,1,0,2,3:T(2,128)(2,1)S(1)} %reshape.15) | data formatting | bytes 4194304 | tf_op jit(solution)/shard_map/reshape | solution.py:241
  42.1 3.2 %reshape.16 = bf16[16,64,1024]{2,1,0:T(8,128)(2,1)S(1)} reshape(bf16[16,16,4,2,512]{4,3,2,1,0:T(2,128)(2,1)} %bitcast.54) | data formatting | bytes 4194304 | tf_op jit(solution)/shard_map/reshape | solution.py:241
  45.3 1.7 pad_maximum_fusion.q_hbm
  47.0 154.6 %attend.1 = bf16[32,64,512]{2,1,0:T(8,128)(2,1)} custom-call(s32[32]{0:T(128)} %lens_ref.1, bf16[16,64,1152]{2,1,0:T(8,128)(2,1)} %pad_maximum_fusion.q_hbm, bf16[32,4096,512]{2,1,0:T(8,128)(2,1)} %kv_hbm.1, bf16[32,64,4096]{2,1,0:T(8,128)(2,1)} %bitcast.52), custom_call_target="tpu_custom_call" | custom-call | tf_op jit(solution)/shard_map/attend/pallas_call | solution.py:206
  201.6 2.6 reshape.19
  204.2 13.2 %fusion.6 = f32[32,4,6144]{2,0,1:T(8,128)} fusion(bf16[16,128,6144]{2,1,0:T(8,128)(2,1)} %param.17, bf16[16,512,128]{2,1,0:T(8,128)(2,1)} %param.16, bf16[32,4,16,512]{3,1,2,0:T(4,128)(2,1)S(1)} %bitcast.53), kind=kOutput, calls=%fused_computation.6 | convolution fusion | flops 3489923072 | bytes 32505856 | tf_op jit(solution)/shard_map/criw,iwe->cre/dot_general | solution.py:247
  217.4 0.0 all-reduce.2.cloned.1.call-update
  217.4 64.4 %all-reduce.2.cloned.1.call-done = f32[32,4,6144]{2,0,1:T(8,128)} async-done(((f32[32,4,6144]{2,0,1:T(8,128)}), f32[32,4,6144]{2,0,1:T(8,128)}) %all-reduce.2.cloned.1.call-update) | async-done | bytes 3145744 | tf_op jit(solution)/shard_map/psum | solution.py:248
  281.7 0.0 copy-start.1
  281.8 3.5 %add_convert_fusion = bf16[32,4,6144]{2,0,1:T(8,128)(2,1)S(1)} fusion(f32[32,4,6144]{2,0,1:T(8,128)} %all-reduce.2.cloned.1.call-done, bf16[32,4,6144]{2,1,0:T(4,128)(2,1)} %param.9), kind=kLoop, calls=%fused_computation.7 | loop fusion | flops 2359296 | bytes 6291456 | tf_op jit(solution)/shard_map/convert_element_type | solution.py:249
  285.2 2.4 copy.14
  287.6 0.0 copy-done.1
Async XLA Ops:
  6.5 27.4 %copy-start = (bf16[16,128,512]{2,1,0:T(8,128)(2,1)S(1)}, bf16[16,128,512]{2,1,0:T(8,128)(2,1)}, u32[]{:S(2)}) copy-start(bf16[16,128,512]{2,1,0:T(8,128)(2,1)} %param.15) | copy-start | bytes 6291460
  6.5 275.2 %all-reduce.2.cloned.1.call-start = ((), (), s32[]{:S(2)}) async-start(), calls=%async_computation | async-start | bytes 6291456 | tf_op jit(solution)/shard_map/psum | solution.py:248
  6.5 17.7 %copy-start.2 = (bf16[32,4,6144]{2,1,0:T(4,128)(2,1)S(1)}, bf16[32,4,6144]{2,1,0:T(4,128)(2,1)}, u32[]{:S(2)}) copy-start(bf16[32,4,6144]{2,1,0:T(4,128)(2,1)} %param.9) | copy-start | bytes 4718596
  281.7 5.9 %copy-start.1 = (bf16[16,128,512]{2,1,0:T(8,128)(2,1)S(1)}, bf16[16,128,512]{2,1,0:T(8,128)(2,1)}, u32[]{:S(2)}) copy-start(bf16[16,128,512]{2,1,0:T(8,128)(2,1)} %param.15) | copy-start | bytes 6291460
Sparse Core Ops, SparseCore 0:
  217.5 64.1 all-reduce.1

commit v2 on v1

--- a/solution.py
+++ b/solution.py
@@ -169,19 +169,30 @@
     lax.fori_loop(0, rows, body, 0)
     merge_side(rows - 1)
 
-    def finish(row, carry):
-        for copy in cross_o(row):
-            copy.wait_recv()
-        pad = jnp.zeros((120, 128), jnp.float32)
-        mine = jnp.transpose(jnp.concatenate([xstat[row], pad], axis=0))[:group]
-        theirs = jnp.transpose(jnp.concatenate([xrstat[row], pad], axis=0))[group:]
-        top_a, top_b = mine[:, 0:1], theirs[:, 0:1]
-        new_top = jnp.maximum(top_a, top_b)
-        keep_a, keep_b = jnp.exp2(top_a - new_top), jnp.exp2(top_b - new_top)
-        total = mine[:, 1:2] * keep_a + theirs[:, 1:2] * keep_b
-        o_ref[row] = ((own[row] * keep_a + xrecv[row] * keep_b) / total).astype(o_ref.dtype)
-        return carry
-    lax.fori_loop(0, rows, finish, 0)
+    def finish(step, carry):
+        parts = []
+        for n in range(4):
+            row = 4 * step + n
+            for copy in cross_o(row):
+                copy.wait_recv()
+            pad = jnp.zeros((120, 128), jnp.float32)
+            mine = jnp.transpose(jnp.concatenate([xstat[row], pad], axis=0))[:group]
+            theirs = jnp.transpose(jnp.concatenate([xrstat[row], pad], axis=0))[group:]
+            top_a, top_b = mine[:, 0:1], theirs[:, 0:1]
+            new_top = jnp.maximum(top_a, top_b)
+            keep_a, keep_b = jnp.exp2(top_a - new_top), jnp.exp2(top_b - new_top)
+            total = mine[:, 1:2] * keep_a + theirs[:, 1:2] * keep_b
+            parts.append(((own[row] * keep_a + xrecv[row] * keep_b) / total).astype(jnp.bfloat16))
+        by_row = jnp.concatenate(parts, axis=0)
+        dst = lax.broadcasted_iota(jnp.int32, (4 * group, 4 * group), 0)
+        src = lax.broadcasted_iota(jnp.int32, (4 * group, 4 * group), 1)
+        head, rest = dst // (4 * toks), lax.rem(dst, 4 * toks)
+        wanted = (rest // toks) * group + head * toks + lax.rem(rest, toks)
+        pick = jnp.where(src == wanted, 1.0, 0.0).astype(jnp.bfloat16)
+        by_head = jnp.dot(pick, by_row, preferred_element_type=jnp.float32).astype(jnp.bfloat16)
+        o_ref[:, pl.ds(pl.multiple_of(step * 4 * toks, 4 * toks), 4 * toks), :] = by_head.reshape(group // toks, 4 * toks, lat)
+        return carry
+    lax.fori_loop(0, rows // 4, finish, 0)
 
     def drain_q(k, carry):
         cross_q(k).wait_send()
@@ -205,7 +216,7 @@
     dma = pltpu.SemaphoreType.DMA
     return pl.pallas_call(
         functools.partial(_attend_kernel, rows, toks, seq_len, score_scale),
-        out_shape=jax.ShapeDtypeStruct((rows, group, lat), bf16),
+        out_shape=jax.ShapeDtypeStruct((group // toks, rows * toks, lat), bf16),
         in_specs=[pl.BlockSpec(memory_space=pltpu.SMEM)] + [pl.BlockSpec(memory_space=pl.ANY)] * 3,
         out_specs=pl.BlockSpec(memory_space=pltpu.VMEM),
         scratch_shapes=[
@@ -229,6 +240,137 @@
     )(lens, q_pack, c_kv, k_rt)
 
 
+def _project_kernel(chunks, o_ref, wuv_ref, hid_ref, wo_hbm, out_ref, ov, rel, hrel, wbuf, ybuf, sbuf, ybin, xbuf, fin,
+                    w_sem, s_sem, x_sem, b_sem, c_sem, f_sem):
+    me = lax.axis_index("seq")
+    side = me + 1 - 2 * lax.rem(me, 2)
+    cross = lax.rem(me + 2, 4)
+    diag = lax.rem(side + 2, 4)
+    heads = o_ref.shape[0]
+    tokens = o_ref.shape[1]
+    val = wuv_ref.shape[2]
+    part = tokens // 4
+    width = wbuf.shape[2]
+    toks = out_ref.shape[1]
+
+    def to(dev):
+        return {"seq": dev}
+
+    def fetch(j):
+        return pltpu.make_async_copy(wo_hbm.at[:, pl.ds(j * width, width)], wbuf.at[j], w_sem.at[j])
+
+    def side_y(j):
+        return pltpu.make_async_remote_copy(ybuf.at[j, pl.ds(2 * part, 2 * part)], sbuf.at[j], s_sem.at[0, j], s_sem.at[1, j],
+                                            device_id=to(side), device_id_type=MESH)
+
+    def cross_y(j):
+        return pltpu.make_async_remote_copy(ybin.at[j], xbuf.at[j], x_sem.at[0, j], x_sem.at[1, j],
+                                            device_id=to(cross), device_id_type=MESH)
+
+    def side_fin(j):
+        return pltpu.make_async_remote_copy(fin.at[j, 0], fin.at[j, 2], b_sem.at[0, j], b_sem.at[1, j],
+                                            device_id=to(side), device_id_type=MESH)
+
+    def cross_fin(j):
+        return pltpu.make_async_remote_copy(fin.at[j, 0], fin.at[j, 1], c_sem.at[0, j], c_sem.at[1, j],
+                                            device_id=to(cross), device_id_type=MESH)
+
+    def fwd_fin(j):
+        return pltpu.make_async_remote_copy(fin.at[j, 1], fin.at[j, 3], f_sem.at[0, j], f_sem.at[1, j],
+                                            device_id=to(side), device_id_type=MESH)
+
+    for j in range(chunks):
+        fetch(j).start()
+    barrier = pltpu.get_barrier_semaphore()
+    for dev in (side, cross, diag):
+        pl.semaphore_signal(barrier, inc=1, device_id=to(dev), device_id_type=MESH)
+    for h in range(heads):
+        ov[:, h * val:(h + 1) * val] = jnp.dot(o_ref[h], wuv_ref[h], preferred_element_type=jnp.float32).astype(jnp.bfloat16)
+    for n, dev in enumerate((me, cross, side, diag)):
+        rows_of = pl.ds(pl.multiple_of(dev * part, part), part)
+        rel[n * part:(n + 1) * part, :] = ov[rows_of, :]
+    hrel[...] = hid_ref[pl.ds(pl.multiple_of(me * part, part), part), :]
+    pl.semaphore_wait(barrier, 3)
+
+    def stage_sum(j):
+        side_y(j).wait_recv()
+        both = ybuf[j, :2 * part] + sbuf[j]
+        ybuf[j, :part] = both[:part]
+        ybin[j] = both[part:]
+        cross_y(j).start()
+
+    def stage_fin(j):
+        cross_y(j).wait_recv()
+        cols = slice(j * width, (j + 1) * width)
+        y = ybuf[j, :part] + xbuf[j]
+        fin[j, 0] = (hrel[:, cols].astype(jnp.float32) + y).astype(jnp.bfloat16)
+        side_fin(j).start()
+        cross_fin(j).start()
+
+    def stage_fwd(j):
+        cross_fin(j).wait_recv()
+        fwd_fin(j).start()
+
+    def stage_out(j):
+        side_fin(j).wait_recv()
+        fwd_fin(j).wait_recv()
+        cols = slice(j * width, (j + 1) * width)
+        for n, dev in enumerate((me, cross, side, diag)):
+            block = fin[j, n].reshape(part // toks, toks, width)
+            out_ref[pl.ds(dev * (part // toks), part // toks), :, cols] = block
+
+    for j in range(chunks + 5):
+        if j < chunks:
+            fetch(j).wait()
+            ybuf[j] = jnp.dot(rel[...], wbuf[j], preferred_element_type=jnp.float32)
+            side_y(j).start()
+        if 1 <= j <= chunks:
+            stage_sum(j - 1)
+        if 3 <= j < chunks + 3:
+            stage_fin(j - 3)
+        if 4 <= j < chunks + 4:
+            stage_fwd(j - 4)
+        if j >= 5:
+            stage_out(j - 5)
+    for j in range(chunks):
+        side_y(j).wait_send()
+        cross_y(j).wait_send()
+        side_fin(j).wait_send()
+        cross_fin(j).wait_send()
+        fwd_fin(j).wait_send()
+
+
+def _project(o_lat, w_uv, hidden, w_o, chunks):
+    rows, toks, model = hidden.shape
+    heads, tokens, lat = o_lat.shape
+    depth = w_o.shape[0]
+    width = model // chunks
+    part = tokens // 4
+    f32, bf16 = jnp.float32, jnp.bfloat16
+    dma = pltpu.SemaphoreType.DMA
+    vmem = pl.BlockSpec(memory_space=pltpu.VMEM)
+    return pl.pallas_call(
+        functools.partial(_project_kernel, chunks),
+        out_shape=jax.ShapeDtypeStruct((rows, toks, model), bf16),
+        in_specs=[vmem, vmem, vmem, pl.BlockSpec(memory_space=pl.ANY)],
+        out_specs=vmem,
+        scratch_shapes=[
+            pltpu.VMEM((tokens, depth), bf16),
+            pltpu.VMEM((tokens, depth), bf16),
+            pltpu.VMEM((part, model), bf16),
+            pltpu.VMEM((chunks, depth, width), bf16),
+            pltpu.VMEM((chunks, tokens, width), f32),
+            pltpu.VMEM((chunks, 2 * part, width), f32),
+            pltpu.VMEM((chunks, part, width), f32),
+            pltpu.VMEM((chunks, part, width), f32),
+            pltpu.VMEM((chunks, 4, part, width), bf16),
+            dma((chunks,)), dma((2, chunks)), dma((2, chunks)), dma((2, chunks)), dma((2, chunks)), dma((2, chunks)),
+        ],
+        compiler_params=pltpu.CompilerParams(collective_id=1, has_side_effects=True, vmem_limit_bytes=60 * 1024 * 1024),
+        name="project",
+    )(o_lat, w_uv, hidden.reshape(tokens, model), w_o)
+
+
 def solution(mesh):
     def local_step(hidden, cache_lens, c_kv, k_r, w_uq, w_qr, w_uk, w_uv, w_o):
         rows, toks, _ = hidden.shape
@@ -242,11 +384,7 @@
         q_rope = q_rope.reshape(rows // 2, 2, toks, heads, rope).transpose(0, 3, 2, 1, 4).reshape(rows // 2, heads * toks, 2 * rope)
         q_pack = jnp.concatenate([q_lat, q_rope], axis=-1)
         o_lat = _attend(cache_lens, q_pack, c_kv, jnp.swapaxes(k_r, 1, 2), toks, score_scale)
-        o_lat = o_lat.reshape(rows, heads, toks, lat).transpose(0, 2, 1, 3)
-        o_val = jnp.einsum("bqhc,hcv->bqhv", o_lat, w_uv, preferred_element_type=jnp.float32).astype(jnp.bfloat16)
-        y_part = jnp.einsum("criw,iwe->cre", o_val, w_o, preferred_element_type=jnp.float32)
-        y_sum = lax.psum(y_part, "seq")
-        return (hidden.astype(jnp.float32) + y_sum).astype(jnp.bfloat16)
+        return _project(o_lat, w_uv, hidden, w_o.reshape(-1, w_o.shape[2]), 12)
 
     specs_in = (P("batch", None, None), P("batch"), P("batch", "seq", None), P("batch", "seq", None),
                 P(None, "seq", None), P(None, "seq", None), P("seq", None, None), P("seq", None, None),

time: 295 us -> 242 us (0.82)
  waiting for transfers between devices: 64.4 us -> 0 us
  Pallas kernels: 155 us -> 197 us
  between operations: 13.5 us -> 0.09 us
  matrix products: 41.8 us -> 28.7 us
  other arithmetic: 5.16 us -> 1.68 us
    psum x1 -> x0, waiting for transfers between devices: 64.4 us -> none  [local_step(): y_sum = lax.psum(y_part, 'seq')]
    pallas_call x0 -> x1, Pallas kernels: none -> 40.3 us  [_project(): pl.pallas_call(functools.partial(_project_kernel, chunks), out_shape=jax....]
    dot_general x1 -> x0, matrix products: 13.2 us -> none  [local_step(): jnp.einsum('criw,iwe->cre', o_val, w_o, preferred_element_type=jnp.float32)]
    convert_element_type x1 -> x0, other arithmetic: 3.49 us -> none  [local_step(): return (hidden.astype(jnp.float32) + y_sum).astype(jnp.bfloat16)]
    unnamed x6 -> x9, local copies, waits for them, and re-layouts: 0.01 us -> 3.23 us
  transfers between devices with their start and end apart: 1 -> 0, of which waited for: 1 -> 0; matrix products, arithmetic and copies ran while one was open for 0% -> 0% of each run, Pallas kernels for 0% -> 0%
where the time goes in v2:
time: 242 us
  Pallas kernels  197 us (81%)
  matrix products  28.7 us (12%)
  local copies, waits for them, and re-layouts  14.6 us (6%)
    pallas_call x1, Pallas kernels, _attend(): pl.pallas_call(functools.partial(_attend_kernel, rows, toks, seq_len, sco...  156 us
    pallas_call x1, Pallas kernels, _project(): pl.pallas_call(functools.partial(_project_kernel, chunks), out_shape=jax....  40.3 us
    dot_general x1, matrix products, local_step(): jnp.einsum('cre,eil->cril', hidden, w_uq, preferred_element_type=jnp.floa...  17.7 us
    reshape x3, local copies, waits for them, and re-layouts, local_step(): q_lat.reshape(rows // 2, 2, toks, heads, lat).transpose(0, 3, 2, 1, 4)  9.33 us
    dot_general x1, matrix products, local_step(): jnp.einsum('cre,eis->cris', hidden, w_qr, preferred_element_type=jnp.floa...  8.96 us

profile of v2, /device:TPU:0, one launch (start us, length us, event | category | flops | bytes accessed | tf_op | source)
XLA Modules:
  0.0 241.8 jit_solution(3755880147187614939)
XLA Ops:
  0.0 0.0 copy-start
  0.0 0.0 copy-start.2
  0.0 17.7 %fusion.15 = bf16[32,4,16,128]{3,0,1,2:T(8,128)(2,1)S(1)} fusion(bf16[6144,16,128,1]{2,1,0,3:T(8,128)(2,1)} %bitcast.38, bf16[32,4,6144,1]{2,1,0,3:T(4,128)(2,1)} %bitcast.35), kind=kOutput, calls=%fused_computation.12 | convolution fusion | flops 3221487616 | bytes 27262976 | tf_op jit(solution)/shard_map/cre,eil->cril/dot_general | solution.py:380
  17.7 0.0 copy-done.2
  17.7 9.0 %fusion.10 = bf16[32,4,16,64]{3,0,2,1:T(8,128)(2,1)S(1)} fusion(bf16[6144,16,64]{0,2,1:T(8,128)(2,1)} %param.14, bf16[32,4,6144,1]{2,1,0,3:T(4,128)(2,1)S(1)} %bitcast.36), kind=kOutput, calls=%fused_computation.11 | convolution fusion | flops 1610743808 | bytes 14417920 | tf_op jit(solution)/shard_map/cre,eis->cris/dot_general | solution.py:381
  26.7 0.5 copy.34
  27.2 0.2 reshape.21
  27.4 0.0 copy-done
  27.4 2.0 convert_bitcast_fusion
  29.4 2.7 %reshape.18 = bf16[16,2,4,16,512]{4,1,0,2,3:T(2,128)(2,1)S(1)} reshape(bf16[32,4,16,512]{3,0,1,2:T(8,128)(2,1)} %convert_bitcast_fusion) | data formatting | bytes 4194304 | tf_op jit(solution)/shard_map/reshape | solution.py:383
  32.2 3.4 %copy.33 = bf16[16,2,4,16,512]{4,1,2,3,0:T(2,128)(2,1)} copy(bf16[16,2,4,16,512]{4,1,0,2,3:T(2,128)(2,1)S(1)} %reshape.18) | data formatting | bytes 4194304 | tf_op jit(solution)/shard_map/reshape | solution.py:383
  35.6 3.2 %reshape.19 = bf16[16,64,1024]{2,1,0:T(8,128)(2,1)S(1)} reshape(bf16[16,16,4,2,512]{4,3,2,1,0:T(2,128)(2,1)} %bitcast.33) | data formatting | bytes 4194304 | tf_op jit(solution)/shard_map/reshape | solution.py:383
  38.8 1.7 pad_maximum_fusion.q_hbm
  40.5 0.0 copy-start.3
  40.5 156.4 %attend.1.o_ref = bf16[16,128,512]{2,1,0:T(8,128)(2,1)} custom-call(s32[32]{0:T(128)} %lens_ref.1, bf16[16,64,1152]{2,1,0:T(8,128)(2,1)} %pad_maximum_fusion.q_hbm, bf16[32,4096,512]{2,1,0:T(8,128)(2,1)} %kv_hbm.1, bf16[32,64,4096]{2,1,0:T(8,128)(2,1)} %bitcast.32), custom_call_target="tpu_custom_call" | custom-call | tf_op jit(solution)/shard_map/attend/pallas_call | solution.py:217
  196.9 0.0 copy-done.3
  196.9 1.3 reshape.22.hid_ref
  198.2 0.0 copy-start.1
  198.2 40.3 %project.1 = bf16[32,4,6144]{2,1,0:T(4,128)(2,1)} custom-call(bf16[16,128,512]{2,1,0:T(8,128)(2,1)} %attend.1.o_ref, bf16[16,512,128]{2,1,0:T(8,128)(2,1)} %wuv_ref.1, bf16[128,6144]{1,0:T(8,128)(2,1)} %reshape.22.hid_ref, bf16[2048,6144]{1,0:T(8,128)(2,1)} %bitcast.31), custom_call_target="tpu_custom_call" | custom-call | tf_op jit(solution)/shard_map/project/pallas_call | solution.py:352
  238.6 3.2 %copy.36 = bf16[32,4,6144]{2,1,0:T(4,128)(2,1)} copy(bf16[32,4,6144]{2,1,0:T(4,128)(2,1)} %project.1) | data formatting | bytes 3145728
  241.8 0.0 copy-done.1
Async XLA Ops:
  0.0 27.4 %copy-start = (bf16[16,128,512]{2,1,0:T(8,128)(2,1)S(1)}, bf16[16,128,512]{2,1,0:T(8,128)(2,1)}, u32[]{:S(2)}) copy-start(bf16[16,128,512]{2,1,0:T(8,128)(2,1)} %param.15) | copy-start | bytes 6291460
  0.0 17.7 %copy-start.2 = (bf16[32,4,6144]{2,1,0:T(4,128)(2,1)S(1)}, bf16[32,4,6144]{2,1,0:T(4,128)(2,1)}, u32[]{:S(2)}) copy-start(bf16[32,4,6144]{2,1,0:T(4,128)(2,1)} %param.9) | copy-start | bytes 4718596
  40.5 156.4 %copy-start.3 = (bf16[32,4,6144]{2,1,0:T(4,128)(2,1)S(1)}, bf16[32,4,6144]{2,1,0:T(4,128)(2,1)}, u32[]{:S(2)}) copy-start(bf16[32,4,6144]{2,1,0:T(4,128)(2,1)} %param.9) | copy-start | bytes 4718596
  198.2 43.6 %copy-start.1 = (bf16[16,128,512]{2,1,0:T(8,128)(2,1)S(1)}, bf16[16,128,512]{2,1,0:T(8,128)(2,1)}, u32[]{:S(2)}) copy-start(bf16[16,128,512]{2,1,0:T(8,128)(2,1)} %param.15) | copy-start | bytes 6291460
